TPU v7x, 32 devices: a whole 2x2x4 slice. The times are simulated.
32 devices in a mesh: mkt: 8 (over z, x), grp: 4 (over y, core).
Axes of the slice: x: 2, y: 2, z: 4, core: 2. Of those that a mesh axis runs over, the one named last changes fastest.
Arguments:
- mean_utility: float32 [512, 64], P(('mkt', 'grp')), may hold values from -5 to -1
- market_share: float32 [512, 64], P(('mkt', 'grp')), may hold values from 0.001 to 0.02
- product_traits: float32 [512, 64, 5], P(('mkt', 'grp')), may hold values from -1 to 1
- taste_draws: float32 [512, 5, 1024], P(('mkt', 'grp')), may hold values from -4 to 4
- taste_scale: float32 [5], replicated, may hold values from 0.3 to 1
- type_weight: float32 [512, 1024], P(('mkt', 'grp')), may hold values from 0.1 to 1
- market_size: float32 [512], P(('mkt', 'grp')), may hold values from 0.05 to 3
- product_firm: int32 [512, 64], P(('mkt', 'grp')), may hold values from 0 to 511, all different within a row
- firm_order: int32 [512], replicated, may hold values from 0 to 511, each once
- loyalty: float32 [512, 1024], P(('mkt', 'grp')), may hold values from -1 to 1
- firm_share: float32 [512, 1024], replicated, may hold values from 2e-05 to 0.15
Outputs:
- utility_out: float32 [512, 64], P(('mkt', 'grp'))
- loyalty_out: float32 [512, 1024], P(('mkt', 'grp'))
Inputs may be any that keep to these rules, and one draw needn't show every extreme that they name: `product_firm`: in each market the 64 products belong to 64 different firms, and every firm sells in some market. `firm_order`: each firm appears once.
All inputs are finite; a program needn't handle non-finite values.
Results may differ from a plain program's by a relative error of at most 0.0001.
Values sent between devices are 32-bit elements; how exact they have to be, the bound alone decides.
A program may use at most 64 MiB of HBM per device.

v0:
```python
import jax
import jax.numpy as jnp
from jax import lax
from jax.sharding import PartitionSpec as P

ITERS = 3
clip_target = 0.5
norm_eps = 1e-06


def inverse_order(firm_order):
    count = firm_order.shape[0]
    return jnp.zeros((count,), jnp.int32).at[firm_order].set(jnp.arange(count, dtype=jnp.int32))


def market_terms(mean_now, taste, type_weight, mass, row_ids, table):
    expu = jnp.exp(mean_now[:, :, None] + taste + jnp.take(table, row_ids, axis=0))
    choice_prob = expu / (1.0 + jnp.sum(expu, axis=1, keepdims=True))
    weighted_sum = jnp.einsum(
        "mjr,mr->mj", choice_prob, type_weight, precision=lax.Precision.HIGHEST
    )
    weighted = choice_prob * mass[:, None, :]
    firm_count = table.shape[0]
    onehot = (
        jnp.arange(firm_count, dtype=jnp.int32)[:, None] == row_ids.reshape(-1)[None, :]
    ).astype(jnp.float32)
    partial_value = jnp.dot(
        onehot,
        weighted.reshape(-1, weighted.shape[2]),
        precision=lax.Precision.HIGHEST,
        preferred_element_type=jnp.float32,
    )
    return (weighted_sum, partial_value)


def local(
    mean_utility,
    market_share,
    product_traits,
    taste_draws,
    taste_scale,
    type_weight,
    market_size,
    product_firm,
    firm_order,
    loyalty,
    firm_share,
):
    firm_count = firm_share.shape[0]
    draw_count = firm_share.shape[1]
    owned_count = loyalty.shape[0]
    devices = lax.axis_size(("mkt", "grp"))
    inverse = inverse_order(firm_order)
    owner_rows = jnp.take(inverse, product_firm, axis=0)
    owned = loyalty
    my_firms = lax.dynamic_slice_in_dim(
        firm_order, lax.axis_index(("mkt", "grp")) * owned_count, owned_count
    )
    taste = jnp.einsum(
        "mjk,mkr->mjr", product_traits * taste_scale, taste_draws, precision=lax.Precision.HIGHEST
    )
    weight_total = jnp.sum(type_weight, axis=1)
    mass = market_size[:, None] * type_weight
    type_mass = lax.psum(jnp.sum(mass, axis=0), ("mkt", "grp"))
    log_observed = jnp.log(market_share)
    mean_now = mean_utility
    my_share = jnp.log(jnp.take(firm_share, my_firms, axis=0))
    for step in range(ITERS):
        table = lax.all_gather(owned, ("mkt", "grp"), axis=0, tiled=True)
        weighted_sum, by_owner = market_terms(mean_now, taste, type_weight, mass, owner_rows, table)
        predicted = weighted_sum / weight_total[:, None]
        blocks = by_owner.reshape(devices, owned_count, draw_count)
        received = lax.all_to_all(blocks, ("mkt", "grp"), split_axis=0, concat_axis=0, tiled=True)
        own_totals = jnp.sum(received, axis=0)
        gap = my_share - jnp.log(own_totals / type_mass[None, :])
        squares = lax.psum(jnp.sum(gap * gap), ("mkt", "grp"))
        clip = jnp.minimum(
            1.0, clip_target / jnp.sqrt(squares / (firm_count * draw_count) + norm_eps)
        )
        owned = owned + clip * gap
        mean_now = mean_now + log_observed - jnp.log(predicted)
    return (mean_now, owned)


def solution(mesh):
    placed = (
        P(("mkt", "grp"), None),
        P(("mkt", "grp"), None),
        P(("mkt", "grp"), None, None),
        P(("mkt", "grp"), None, None),
        P(),
        P(("mkt", "grp"), None),
        P(("mkt", "grp")),
        P(("mkt", "grp"), None),
        P(),
        P(("mkt", "grp"), None),
        P(),
    )
    return jax.shard_map(
        local,
        mesh=mesh,
        in_specs=placed,
        out_specs=(P(("mkt", "grp"), None), P(("mkt", "grp"), None)),
        check_vma=False,
    )
```

profile of v0, /device:TPU:12, one launch (start us, length us, event | category | flops | bytes accessed | tf_op | source)
XLA Modules:
  0.0 555.5 jit_solution(14951167932557971051)
XLA Ops:
  11.9 6.9 %gather_fusion = s32[1024]{0:T(1024)S(1)} fusion(s32[512]{0:T(512)S(1)} %scatter_custom_fusion, s32[1024]{0:T(1024)S(1)} %broadcast_clamp_fusion.1), kind=kCustom, calls=%fused_computation.3 | custom fusion | bytes 12288 | tf_op jit(solution)/shard_map/jit(_take)/gather | solution.py:54
  19.1 48.2 %all-gather.4.cloned.1.call-done = f32[512,1024]{1,0:T(8,128)} async-done(((f32[16,1024]{1,0:T(8,128)}), f32[512,1024]{1,0:T(8,128)}) %all-gather.4.cloned.1.call-update) | async-done | bytes 2097168 | tf_op jit(solution)/shard_map/all_gather | solution.py:69
  67.3 8.0 %gather_fusion.2 = f32[1024,1024]{1,0:T(8,128)} fusion(f32[512,1024]{1,0:T(8,128)} %all-gather.4.cloned.1.call-done, s32[1024]{0:T(1024)S(1)} %broadcast_clamp_fusion), kind=kCustom, calls=%fused_computation.clone | custom fusion | bytes 8392704 | tf_op jit(solution)/shard_map/jit(_take)/gather | solution.py:17
  75.3 7.5 %fusion.31 = (f32[16,1024]{1,0:T(8,128)S(1)}, f32[16,64,1024]{2,1,0:T(8,128)S(1)}, f32[16,64,1024]{2,1,0:T(8,128)}) fusion(f32[16,64,1024]{2,1,0:T(8,128)} %bitcast.24, pred[16,64]{1,0:T(8,128)(4,1)S(1)} %get-tuple-element.19, f32[16,64]{1,0:T(8,128)S(1)} %copy-done.11, f32[16,5,1024]{2,0,1:T(8,128)S(1)} %copy-done.4, ...), kind=kOutput, calls=%fused_computation.73 | convolution fusion | flops 67092480 | bytes 13001728 | tf_op jit(solution)/shard_map/mjk,mkr->mjr/dot_general | solution.py:59
  85.2 5.0 fusion.7
  90.2 4.7 all-to-all-start
  96.4 66.8 %psum.28 = f32[1024]{0:T(1024)S(1)} all-reduce(f32[1024]{0:T(1024)S(1)} %get-tuple-element.15), channel_id=1, replica_groups=mesh['mkt'=8,'grp'=4] {'mkt','grp'}, use_global_device_ids=true, to_apply=%region_5.7 | all-reduce | flops 1024 | bytes 8192 | tf_op jit(solution)/shard_map/psum | solution.py:64
  165.6 40.8 %psum.29 = f32[]{:T(128)} all-reduce(f32[]{:T(128)} %get-tuple-element.11), channel_id=1, replica_groups=mesh['mkt'=8,'grp'=4] {'mkt','grp'}, use_global_device_ids=true, to_apply=%region_7.9 | all-reduce | flops 1 | bytes 8 | tf_op jit(solution)/shard_map/psum | solution.py:76
  207.9 5.5 fusion.9
  213.6 49.5 %all-gather.6.cloned.1.call-done = f32[512,1024]{1,0:T(8,128)} async-done(((f32[16,1024]{1,0:T(8,128)}), f32[512,1024]{1,0:T(8,128)}) %all-gather.6.cloned.1.call-update) | async-done | bytes 2097168 | tf_op jit(solution)/shard_map/all_gather | solution.py:69
  263.0 8.0 %gather_fusion.3 = f32[1024,1024]{1,0:T(8,128)} fusion(f32[512,1024]{1,0:T(8,128)} %all-gather.6.cloned.1.call-done, s32[1024]{0:T(1024)S(1)} %broadcast_clamp_fusion), kind=kCustom, calls=%fused_computation.1.clone | custom fusion | bytes 8392704 | tf_op jit(solution)/shard_map/jit(_take)/gather | solution.py:17
  271.0 4.0 fusion.28
  277.4 3.7 fusion.5
  281.2 51.7 %all_to_all.15 = f32[32,16,1024]{2,1,0:T(8,128)} all-to-all(f32[32,16,1024]{2,1,0:T(8,128)S(1)} %fusion.5), channel_id=1, replica_groups=mesh['mkt'=8,'grp'=4] {'mkt','grp'}, dimensions={0} | all-to-all | bytes 4194304 | tf_op jit(solution)/shard_map/all_to_all | solution.py:73
  335.3 41.9 %psum.30 = f32[]{:T(128)} all-reduce(f32[]{:T(128)} %get-tuple-element.7), channel_id=1, replica_groups=mesh['mkt'=8,'grp'=4] {'mkt','grp'}, use_global_device_ids=true, to_apply=%region_11.13 | all-reduce | flops 1 | bytes 8 | tf_op jit(solution)/shard_map/psum | solution.py:76
  378.5 5.5 fusion.10
  384.1 48.1 %all-gather.8.cloned.1.call-done = f32[512,1024]{1,0:T(8,128)} async-done(((f32[16,1024]{1,0:T(8,128)}), f32[512,1024]{1,0:T(8,128)}) %all-gather.8.cloned.1.call-update) | async-done | bytes 2097168 | tf_op jit(solution)/shard_map/all_gather | solution.py:69
  432.2 8.0 %gather_fusion.4 = f32[1024,1024]{1,0:T(8,128)} fusion(f32[512,1024]{1,0:T(8,128)} %all-gather.8.cloned.1.call-done, s32[1024]{0:T(1024)S(1)} %broadcast_clamp_fusion), kind=kCustom, calls=%fused_computation.2.clone | custom fusion | bytes 8392704 | tf_op jit(solution)/shard_map/jit(_take)/gather | solution.py:17
  440.3 4.1 fusion.26
  446.6 5.0 fusion.3
  451.7 4.7 all-to-all-start.2
  456.4 5.5 fusion.11
  462.7 40.2 %all-to-all-done.2 = f32[32,16,1024]{2,1,0:T(8,128)} async-done(((f32[32,16,1024]{2,1,0:T(8,128)}), f32[32,16,1024]{2,1,0:T(8,128)}, u32[]{:S(2)}, u32[]{:S(2)}) %all-to-all-start.2) | async-done | bytes 2097184 | tf_op jit(solution)/shard_map/all_to_all | solution.py:73
  505.3 42.4 %psum.31 = f32[]{:T(128)} all-reduce(f32[]{:T(128)} %get-tuple-element.3), channel_id=1, replica_groups=mesh['mkt'=8,'grp'=4] {'mkt','grp'}, use_global_device_ids=true, to_apply=%region_15.17 | all-reduce | flops 1 | bytes 8 | tf_op jit(solution)/shard_map/psum | solution.py:76
  (72 shorter events, 23.7 us)
Async XLA Ops:
  7.2 88.6 %copy-start = (f32[512,1024]{1,0:T(8,128)S(1)}, f32[512,1024]{1,0:T(8,128)}, u32[]{:S(2)}) copy-start(f32[512,1024]{1,0:T(8,128)} %param.23) | copy-start | bytes 6291460
  7.2 60.1 %all-gather.4.cloned.1.call-start = ((), (), s32[]{:S(2)}) async-start(), calls=%async_computation.3 | async-start | bytes 2162688 | tf_op jit(solution)/shard_map/all_gather | solution.py:69
  11.8 7.0 %copy-start.12 = (s32[16,64]{1,0:T(8,128)S(1)}, s32[16,64]{1,0:T(8,128)}, u32[]{:S(2)}) copy-start(s32[16,64]{1,0:T(8,128)} %param.20) | copy-start | bytes 12292
  11.8 7.1 %copy-start.10 = (f32[16,64,5]{1,0,2:T(8,128)S(1)}, f32[16,64,5]{1,0,2:T(8,128)}, u32[]{:S(2)}) copy-start(f32[16,64,5]{1,0,2:T(8,128)} %param.15) | copy-start | bytes 61444
  11.9 7.1 %copy-start.13 = (f32[5]{0:T(128)S(1)}, f32[5]{0:T(128)}, u32[]{:S(2)}) copy-start(f32[5]{0:T(128)} %param.17) | copy-start | bytes 64
  19.1 56.2 %copy-start.4 = (f32[16,5,1024]{2,0,1:T(8,128)S(1)}, f32[16,5,1024]{2,0,1:T(8,128)}, u32[]{:S(2)}) copy-start(f32[16,5,1024]{2,0,1:T(8,128)} %param.16) | copy-start | bytes 983044
  19.1 56.2 %copy-start.11 = (f32[16,64]{1,0:T(8,128)S(1)}, f32[16,64]{1,0:T(8,128)}, u32[]{:S(2)}) copy-start(f32[16,64]{1,0:T(8,128)} %param.13) | copy-start | bytes 12292
  75.3 7.5 %copy-start.9 = (f32[16,1024]{1,0:T(8,128)S(1)}, f32[16,1024]{1,0:T(8,128)}, u32[]{:S(2)}) copy-start(f32[16,1024]{1,0:T(8,128)} %param.18) | copy-start | bytes 196612
  75.3 7.5 %copy-start.14 = (f32[16]{0:T(128)S(1)}, f32[16]{0:T(128)}, u32[]{:S(2)}) copy-start(f32[16]{0:T(128)} %param.19) | copy-start | bytes 196
  82.9 2.4 copy-start.1
  90.2 116.8 %copy-start.7 = (f32[16,1024]{1,0:T(8,128)S(1)}, f32[16,1024]{1,0:T(8,128)}, u32[]{:S(2)}) copy-start(f32[16,1024]{1,0:T(8,128)} %param.22) | copy-start | bytes 196612
  90.2 72.9 %all-to-all-start = ((f32[32,16,1024]{2,1,0:T(8,128)}), f32[32,16,1024]{2,1,0:T(8,128)}, u32[]{:S(2)}, u32[]{:S(2)}) async-start(f32[32,16,1024]{2,1,0:T(8,128)} %fusion.7), calls=%async_computation | async-start | bytes 4194304 | tf_op jit(solution)/shard_map/all_to_all | solution.py:73
  95.0 168.1 %all-gather.6.cloned.1.call-start = ((), (), s32[]{:S(2)}) async-start(), calls=%async_computation.4 | async-start | bytes 2162688 | tf_op jit(solution)/shard_map/all_gather | solution.py:69
  207.7 224.5 %all-gather.8.cloned.1.call-start = ((), (), s32[]{:S(2)}) async-start(), calls=%async_computation.5 | async-start | bytes 2162688 | tf_op jit(solution)/shard_map/all_gather | solution.py:69
  207.9 5.5 copy-start.8
  275.1 2.3 copy-start.2
  281.2 96.7 %copy-start.6 = (f32[16,1024]{1,0:T(8,128)S(1)}, f32[16,1024]{1,0:T(8,128)}, u32[]{:S(2)}) copy-start(f32[16,1024]{1,0:T(8,128)} %multiply_add_fusion.2) | copy-start | bytes 196612
  444.3 2.3 copy-start.3
  451.7 51.2 %all-to-all-start.2 = ((f32[32,16,1024]{2,1,0:T(8,128)}), f32[32,16,1024]{2,1,0:T(8,128)}, u32[]{:S(2)}, u32[]{:S(2)}) async-start(f32[32,16,1024]{2,1,0:T(8,128)} %fusion.3), calls=%async_computation.2 | async-start | bytes 4194304 | tf_op jit(solution)/shard_map/all_to_all | solution.py:73
  456.4 91.9 %copy-start.5 = (f32[16,1024]{1,0:T(8,128)S(1)}, f32[16,1024]{1,0:T(8,128)}, u32[]{:S(2)}) copy-start(f32[16,1024]{1,0:T(8,128)} %multiply_add_fusion.1) | copy-start | bytes 196612
Sparse Core Ops, SparseCore 0:
  10.8 56.4 all-gather.3
  207.8 55.1 all-gather.5
  378.7 53.5 all-gather.7
where the time goes:
time: 557 us; the launch traced here: 556 us
  blocking collectives  244 us (44%)
  waiting for transfers between devices  187 us (34%)
  local copies, waits for them, and re-layouts  38.1 us (7%)
  matrix products  37.9 us (7%)
  other arithmetic  23.5 us (4%)
  between operations  16 us (3%)
  starting transfers between devices  9.77 us (2%)
    all_gather x3, waiting for transfers between devices, local(): table = lax.all_gather(owned, ('mkt', 'grp'), axis=0, tiled=True)  146 us
    psum x3, blocking collectives, local(): squares = lax.psum(jnp.sum(gap * gap), ('mkt', 'grp'))  125 us
    psum x1, blocking collectives, local(): type_mass = lax.psum(jnp.sum(mass, axis=0), ('mkt', 'grp'))  66.8 us
    all_to_all x1, blocking collectives, local(): lax.all_to_all(blocks, ('mkt', 'grp'), split_axis=0, concat_axis=0, tiled...  51.7 us
    all_to_all x2, waiting for transfers between devices, local(): lax.all_to_all(blocks, ('mkt', 'grp'), split_axis=0, concat_axis=0, tiled...  40.2 us
    gather x3, local copies, waits for them, and re-layouts, market_terms(): jnp.take(table, row_ids, axis=0)  24 us
    dot_general x3, matrix products, market_terms(): jnp.einsum('mjr,mr->mj', choice_prob, type_weight, precision=lax.Precisio...  16.6 us
    dot_general x3, matrix products, market_terms(): jnp.dot(onehot, weighted.reshape(-1, weighted.shape[2]), precision=lax.Pr...  13.8 us
  transfers between devices with their start and end apart: 5, of which 4 were waited for; matrix products, arithmetic and copies ran while one was open for 5% of the time, Pallas kernels for 0%

commit v1 on v0

--- a/solution.py
+++ b/solution.py
@@ -66,7 +66,12 @@
     mean_now = mean_utility
     my_share = jnp.log(jnp.take(firm_share, my_firms, axis=0))
     for step in range(ITERS):
-        table = lax.all_gather(owned, ("mkt", "grp"), axis=0, tiled=True)
+        table = jnp.concatenate(
+            lax.all_to_all(
+                jnp.stack([owned] * lax.axis_size(("mkt", "grp"))), ("mkt", "grp"), 0, 0
+            ),
+            axis=0,
+        )
         weighted_sum, by_owner = market_terms(mean_now, taste, type_weight, mass, owner_rows, table)
         predicted = weighted_sum / weight_total[:, None]
         blocks = by_owner.reshape(devices, owned_count, draw_count)

time: 557 us -> 530 us (0.952)
  waiting for transfers between devices: 187 us -> 158 us
  starting transfers between devices: 9.77 us -> 26.8 us
  between operations: 16 us -> 3.03 us
    all_gather x3 -> x0, waiting for transfers between devices: 146 us -> none  [local(): table = lax.all_gather(owned, ('mkt', 'grp'), axis=0, tiled=True)]
    all_to_all x0 -> x3, waiting for transfers between devices: none -> 118 us  [local(): lax.all_to_all(jnp.stack([owned] * lax.axis_size(('mkt', 'grp'))), ('mkt'...]
    all_to_all x0 -> x3, starting transfers between devices: none -> 14 us  [local(): lax.all_to_all(jnp.stack([owned] * lax.axis_size(('mkt', 'grp'))), ('mkt'...]
    another operation x0 -> x3, local copies, waits for them, and re-layouts: none -> 5.82 us  [local(): jnp.stack([owned] * lax.axis_size(('mkt', 'grp')))]
where the time goes in v1:
time: 530 us; the launch traced here: 529 us
  blocking collectives  246 us (46%)
  waiting for transfers between devices  158 us (30%)
  local copies, waits for them, and re-layouts  38.8 us (7%)
  matrix products  38 us (7%)
  starting transfers between devices  26.8 us (5%)
  other arithmetic  18.5 us (3%)
    psum x3, blocking collectives, local(): squares = lax.psum(jnp.sum(gap * gap), ('mkt', 'grp'))  125 us
    all_to_all x3, waiting for transfers between devices, local(): lax.all_to_all(jnp.stack([owned] * lax.axis_size(('mkt', 'grp'))), ('mkt'...  118 us
    psum x1, blocking collectives, local(): type_mass = lax.psum(jnp.sum(mass, axis=0), ('mkt', 'grp'))  67.5 us
    all_to_all x1, blocking collectives, local(): lax.all_to_all(blocks, ('mkt', 'grp'), split_axis=0, concat_axis=0, tiled...  53.2 us
    all_to_all x2, waiting for transfers between devices, local(): lax.all_to_all(blocks, ('mkt', 'grp'), split_axis=0, concat_axis=0, tiled...  40.1 us
    gather x3, local copies, waits for them, and re-layouts, market_terms(): jnp.take(table, row_ids, axis=0)  18.9 us
    dot_general x3, matrix products, market_terms(): jnp.einsum('mjr,mr->mj', choice_prob, type_weight, precision=lax.Precisio...  16.7 us
    all_to_all x3, starting transfers between devices, local(): lax.all_to_all(jnp.stack([owned] * lax.axis_size(('mkt', 'grp'))), ('mkt'...  14 us
  transfers between devices with their start and end apart: 5, of which 4 were waited for; matrix products, arithmetic and copies ran while one was open for 5% of the time, Pallas kernels for 0%

profile of v1, /device:TPU:12, one launch (start us, length us, event | category | flops | bytes accessed | tf_op | source)
XLA Modules:
  0.0 528.9 jit_solution(6874136523686788930)
XLA Ops:
  3.2 6.0 %all-to-all-start = ((f32[32,16,1024]{2,1,0:T(8,128)}), f32[32,16,1024]{2,1,0:T(8,128)}, u32[]{:S(2)}, u32[]{:S(2)}) async-start(f32[32,16,1024]{2,1,0:T(8,128)} %stack.6), calls=%async_computation | async-start | bytes 4194304 | tf_op jit(solution)/shard_map/all_to_all | solution.py:70
  11.8 6.9 %gather_fusion = s32[1024]{0:T(1024)S(1)} fusion(s32[512]{0:T(512)S(1)} %scatter_custom_fusion, s32[1024]{0:T(1024)S(1)} %broadcast_clamp_fusion.1), kind=kCustom, calls=%fused_computation.3 | custom fusion | bytes 12288 | tf_op jit(solution)/shard_map/jit(_take)/gather | solution.py:54
  19.0 36.6 %all-to-all-done = f32[32,16,1024]{2,1,0:T(8,128)} async-done(((f32[32,16,1024]{2,1,0:T(8,128)}), f32[32,16,1024]{2,1,0:T(8,128)}, u32[]{:S(2)}, u32[]{:S(2)}) %all-to-all-start) | async-done | bytes 2097184 | tf_op jit(solution)/shard_map/all_to_all | solution.py:70
  55.7 8.1 %gather_fusion.2 = f32[1024,1024]{1,0:T(8,128)} fusion(f32[512,1024]{1,0:T(8,128)} %bitcast, s32[1024]{0:T(1024)S(1)} %broadcast_clamp_fusion), kind=kCustom, calls=%fused_computation.clone | custom fusion | bytes 8392704 | tf_op jit(solution)/shard_map/jit(_take)/gather | solution.py:17
  63.8 7.5 %fusion.31 = (f32[16,1024]{1,0:T(8,128)S(1)}, f32[16,64,1024]{2,1,0:T(8,128)S(1)}, f32[16,64,1024]{2,1,0:T(8,128)}) fusion(f32[16,64,1024]{2,1,0:T(8,128)} %bitcast.29, pred[16,64]{1,0:T(8,128)(4,1)S(1)} %get-tuple-element.19, f32[16,64]{1,0:T(8,128)S(1)} %copy-done.10, f32[16,5,1024]{2,0,1:T(8,128)S(1)} %copy-done.5, ...), kind=kOutput, calls=%fused_computation.73 | convolution fusion | flops 67092480 | bytes 13001728 | tf_op jit(solution)/shard_map/mjk,mkr->mjr/dot_general | solution.py:59
  73.7 5.0 fusion.7
  78.7 6.4 %all-to-all-start.1 = ((f32[32,16,1024]{2,1,0:T(8,128)}), f32[32,16,1024]{2,1,0:T(8,128)}, u32[]{:S(2)}, u32[]{:S(2)}) async-start(f32[32,16,1024]{2,1,0:T(8,128)} %fusion.7), calls=%async_computation.1 | async-start | bytes 4194304 | tf_op jit(solution)/shard_map/all_to_all | solution.py:78
  85.8 67.5 %psum.28 = f32[1024]{0:T(1024)S(1)} all-reduce(f32[1024]{0:T(1024)S(1)} %get-tuple-element.15), channel_id=1, replica_groups=mesh['mkt'=8,'grp'=4] {'mkt','grp'}, use_global_device_ids=true, to_apply=%region_5.7 | all-reduce | flops 1024 | bytes 8192 | tf_op jit(solution)/shard_map/psum | solution.py:64
  155.7 40.7 %psum.29 = f32[]{:T(128)} all-reduce(f32[]{:T(128)} %get-tuple-element.11), channel_id=1, replica_groups=mesh['mkt'=8,'grp'=4] {'mkt','grp'}, use_global_device_ids=true, to_apply=%region_7.9 | all-reduce | flops 1 | bytes 8 | tf_op jit(solution)/shard_map/psum | solution.py:81
  198.7 4.8 all-to-all-start.2
  203.5 5.5 %fusion.9 = f32[16,1,64]{2,1,0:T(1,128)S(1)} fusion(f32[16,64,1024]{2,1,0:T(8,128)} %copy-done.2, f32[16,1024]{1,0:T(8,128)S(1)} %get-tuple-element.23, f32[16,1024,1]{1,0,2:T(8,128)S(1)} %bitcast.33), kind=kOutput, calls=%fused_computation.24 | convolution fusion | flops 13631488 | bytes 4329472 | tf_op jit(solution)/shard_map/mjr,mr->mj/dot_general | solution.py:19
  209.1 40.8 %all-to-all-done.2 = f32[32,16,1024]{2,1,0:T(8,128)S(1)} async-done(((f32[32,16,1024]{2,1,0:T(8,128)}), f32[32,16,1024]{2,1,0:T(8,128)S(1)}, u32[]{:S(2)}, u32[]{:S(2)}) %all-to-all-start.2) | async-done | bytes 2097184 | tf_op jit(solution)/shard_map/all_to_all | solution.py:70
  249.9 5.4 %gather_fusion.3 = f32[1024,1024]{1,0:T(8,128)} fusion(f32[512,1024]{1,0:T(8,128)S(1)} %bitcast.28, s32[1024]{0:T(1024)S(1)} %broadcast_clamp_fusion), kind=kCustom, calls=%fused_computation.1.clone | custom fusion | bytes 8392704 | tf_op jit(solution)/shard_map/jit(_take)/gather | solution.py:17
  265.4 53.2 %all_to_all.30 = f32[32,16,1024]{2,1,0:T(8,128)S(1)} all-to-all(f32[32,16,1024]{2,1,0:T(8,128)S(1)} %fusion.5), channel_id=1, replica_groups=mesh['mkt'=8,'grp'=4] {'mkt','grp'}, dimensions={0} | all-to-all | bytes 4194304 | tf_op jit(solution)/shard_map/all_to_all | solution.py:78
  319.5 41.7 %psum.30 = f32[]{:T(128)} all-reduce(f32[]{:T(128)} %get-tuple-element.7), channel_id=1, replica_groups=mesh['mkt'=8,'grp'=4] {'mkt','grp'}, use_global_device_ids=true, to_apply=%region_11.13 | all-reduce | flops 1 | bytes 8 | tf_op jit(solution)/shard_map/psum | solution.py:81
  366.7 5.5 %fusion.10 = f32[16,1,64]{2,1,0:T(1,128)S(1)} fusion(f32[16,64,1024]{2,1,0:T(8,128)} %copy-done.3, f32[16,1024]{1,0:T(8,128)S(1)} %broadcast_add_fusion.1, f32[16,1024,1]{1,0,2:T(8,128)S(1)} %bitcast.34), kind=kOutput, calls=%fused_computation.25 | convolution fusion | flops 13631488 | bytes 4329472 | tf_op jit(solution)/shard_map/mjr,mr->mj/dot_general | solution.py:19
  372.3 40.8 %all-to-all-done.4 = f32[32,16,1024]{2,1,0:T(8,128)S(1)} async-done(((f32[32,16,1024]{2,1,0:T(8,128)}), f32[32,16,1024]{2,1,0:T(8,128)S(1)}, u32[]{:S(2)}, u32[]{:S(2)}) %all-to-all-start.4) | async-done | bytes 2097184 | tf_op jit(solution)/shard_map/all_to_all | solution.py:70
  413.1 5.4 %gather_fusion.4 = f32[1024,1024]{1,0:T(8,128)} fusion(f32[512,1024]{1,0:T(8,128)S(1)} %bitcast.27, s32[1024]{0:T(1024)S(1)} %broadcast_clamp_fusion), kind=kCustom, calls=%fused_computation.2.clone | custom fusion | bytes 8392704 | tf_op jit(solution)/shard_map/jit(_take)/gather | solution.py:17
  418.5 4.0 fusion.26
  424.9 5.0 fusion.3
  429.9 6.4 %all-to-all-start.5 = ((f32[32,16,1024]{2,1,0:T(8,128)}), f32[32,16,1024]{2,1,0:T(8,128)}, u32[]{:S(2)}, u32[]{:S(2)}) async-start(f32[32,16,1024]{2,1,0:T(8,128)} %fusion.3), calls=%async_computation.5 | async-start | bytes 4194304 | tf_op jit(solution)/shard_map/all_to_all | solution.py:78
  436.3 5.7 %fusion.11 = f32[16,1,64]{2,1,0:T(1,128)S(1)} fusion(f32[16,64,1024]{2,1,0:T(8,128)} %copy-done.4, f32[16,1024]{1,0:T(8,128)S(1)} %broadcast_add_fusion, f32[16,1024,1]{1,0,2:T(8,128)S(1)} %bitcast.35), kind=kOutput, calls=%fused_computation.26 | convolution fusion | flops 13631488 | bytes 4329472 | tf_op jit(solution)/shard_map/mjr,mr->mj/dot_general | solution.py:19
  442.7 40.1 %all-to-all-done.5 = f32[32,16,1024]{2,1,0:T(8,128)} async-done(((f32[32,16,1024]{2,1,0:T(8,128)}), f32[32,16,1024]{2,1,0:T(8,128)}, u32[]{:S(2)}, u32[]{:S(2)}) %all-to-all-start.5) | async-done | bytes 2097184 | tf_op jit(solution)/shard_map/all_to_all | solution.py:78
  485.2 42.4 %psum.31 = f32[]{:T(128)} all-reduce(f32[]{:T(128)} %get-tuple-element.3), channel_id=1, replica_groups=mesh['mkt'=8,'grp'=4] {'mkt','grp'}, use_global_device_ids=true, to_apply=%region_15.17 | all-reduce | flops 1 | bytes 8 | tf_op jit(solution)/shard_map/psum | solution.py:81
  (72 shorter events, 34.4 us)
Async XLA Ops:
  0.6 84.5 %copy-start = (f32[512,1024]{1,0:T(8,128)S(1)}, f32[512,1024]{1,0:T(8,128)}, u32[]{:S(2)}) copy-start(f32[512,1024]{1,0:T(8,128)} %param.23) | copy-start | bytes 6291460
  0.6 8.6 %copy-start.11 = (s32[16,64]{1,0:T(8,128)S(1)}, s32[16,64]{1,0:T(8,128)}, u32[]{:S(2)}) copy-start(s32[16,64]{1,0:T(8,128)} %param.20) | copy-start | bytes 12292
  0.7 8.7 %copy-start.12 = (s32[512]{0:T(512)S(1)}, s32[512]{0:T(512)}, u32[]{:S(2)}) copy-start(s32[512]{0:T(512)} %param.21) | copy-start | bytes 6148
  3.2 52.5 %all-to-all-start = ((f32[32,16,1024]{2,1,0:T(8,128)}), f32[32,16,1024]{2,1,0:T(8,128)}, u32[]{:S(2)}, u32[]{:S(2)}) async-start(f32[32,16,1024]{2,1,0:T(8,128)} %stack.6), calls=%async_computation | async-start | bytes 4194304 | tf_op jit(solution)/shard_map/all_to_all | solution.py:70
  11.8 7.1 %copy-start.9 = (f32[16,64,5]{1,0,2:T(8,128)S(1)}, f32[16,64,5]{1,0,2:T(8,128)}, u32[]{:S(2)}) copy-start(f32[16,64,5]{1,0,2:T(8,128)} %param.15) | copy-start | bytes 61444
  11.8 7.1 %copy-start.13 = (f32[5]{0:T(128)S(1)}, f32[5]{0:T(128)}, u32[]{:S(2)}) copy-start(f32[5]{0:T(128)} %param.17) | copy-start | bytes 64
  55.7 8.1 %copy-start.5 = (f32[16,5,1024]{2,0,1:T(8,128)S(1)}, f32[16,5,1024]{2,0,1:T(8,128)}, u32[]{:S(2)}) copy-start(f32[16,5,1024]{2,0,1:T(8,128)} %param.16) | copy-start | bytes 983044
  55.7 8.1 %copy-start.10 = (f32[16,64]{1,0:T(8,128)S(1)}, f32[16,64]{1,0:T(8,128)}, u32[]{:S(2)}) copy-start(f32[16,64]{1,0:T(8,128)} %param.13) | copy-start | bytes 12292
  63.8 7.5 %copy-start.8 = (f32[16,1024]{1,0:T(8,128)S(1)}, f32[16,1024]{1,0:T(8,128)}, u32[]{:S(2)}) copy-start(f32[16,1024]{1,0:T(8,128)} %param.18) | copy-start | bytes 196612
  63.8 7.5 %copy-start.14 = (f32[16]{0:T(128)S(1)}, f32[16]{0:T(128)}, u32[]{:S(2)}) copy-start(f32[16]{0:T(128)} %param.19) | copy-start | bytes 196
  71.3 2.4 copy-start.2
  78.7 118.4 %copy-start.6 = (f32[16,1024]{1,0:T(8,128)S(1)}, f32[16,1024]{1,0:T(8,128)}, u32[]{:S(2)}) copy-start(f32[16,1024]{1,0:T(8,128)} %param.22) | copy-start | bytes 196612
  78.7 74.6 %all-to-all-start.1 = ((f32[32,16,1024]{2,1,0:T(8,128)}), f32[32,16,1024]{2,1,0:T(8,128)}, u32[]{:S(2)}, u32[]{:S(2)}) async-start(f32[32,16,1024]{2,1,0:T(8,128)} %fusion.7), calls=%async_computation.1 | async-start | bytes 4194304 | tf_op jit(solution)/shard_map/all_to_all | solution.py:78
  198.7 51.2 %all-to-all-start.2 = ((f32[32,16,1024]{2,1,0:T(8,128)}), f32[32,16,1024]{2,1,0:T(8,128)S(1)}, u32[]{:S(2)}, u32[]{:S(2)}) async-start(f32[32,16,1024]{2,1,0:T(8,128)} %stack.7), calls=%async_computation.2 | async-start | bytes 4194304 | tf_op jit(solution)/shard_map/all_to_all | solution.py:70
  203.5 5.5 %copy-start.7 = (f32[16,64]{1,0:T(8,128)S(1)}, f32[16,64]{1,0:T(8,128)}, u32[]{:S(2)}) copy-start(f32[16,64]{1,0:T(8,128)} %param.14) | copy-start | bytes 12292
  259.4 2.3 copy-start.3
  363.5 49.5 %all-to-all-start.4 = ((f32[32,16,1024]{2,1,0:T(8,128)}), f32[32,16,1024]{2,1,0:T(8,128)S(1)}, u32[]{:S(2)}, u32[]{:S(2)}) async-start(f32[32,16,1024]{2,1,0:T(8,128)} %stack.8), calls=%async_computation.4 | async-start | bytes 4194304 | tf_op jit(solution)/shard_map/all_to_all | solution.py:70
  422.6 2.3 copy-start.4
  429.9 52.8 %all-to-all-start.5 = ((f32[32,16,1024]{2,1,0:T(8,128)}), f32[32,16,1024]{2,1,0:T(8,128)}, u32[]{:S(2)}, u32[]{:S(2)}) async-start(f32[32,16,1024]{2,1,0:T(8,128)} %fusion.3), calls=%async_computation.5 | async-start | bytes 4194304 | tf_op jit(solution)/shard_map/all_to_all | solution.py:78
  436.3 92.6 %copy-start.1 = (f32[512,1024]{1,0:T(8,128)S(1)}, f32[512,1024]{1,0:T(8,128)}, u32[]{:S(2)}) copy-start(f32[512,1024]{1,0:T(8,128)} %param.23) | copy-start | bytes 6291460
